TPU v7x, 32 devices: a whole 2x2x4 slice. The times are simulated.
32 devices in a mesh: ctx: 16 (over z, y, x), tp: 2 (over core).
Axes of the slice: x: 2, y: 2, z: 4, core: 2. Of those that a mesh axis runs over, the one named last changes fastest.
Arguments:
- byte_states: bfloat16 [4096, 1024], P('ctx'), may hold values from -12 to 12, as said below
- patch_of_byte: int32 [4096], P('ctx'), may hold values from 0 to 125, as said below
- patch_first: int32 [16], replicated, may hold values from 0 to 991, as said below
- moved: int32 [2, 16], replicated, may hold values from 0 to 32, as said below
- w_qkv: bfloat16 [3, 1024, 2048], P(None, None, 'tp'), may hold values from -0.25 to 0.25, as said below
- d_attn: bfloat16 [1024, 2048], P('ctx', 'tp'), may hold values from -6 to 6
Outputs:
- attn_out: bfloat16 [1024, 2048], P('ctx', 'tp')
- byte_grad: bfloat16 [4096, 1024], P('ctx', 'tp')
Inputs may be any that keep to these rules, and one draw needn't show every extreme that they name: `patch_of_byte`: within each byte shard the numbers start at 0 and rise by 0 or 1 from byte to byte; a shard holds at most 126 patches, reached on some shard. `patch_first`: the sum of the patch counts of all earlier byte shards; shard 0 starts at 0. moved[0, 0] = 0 and moved[1, 15] = 0; every other entry is 1 to 32; every patch shard thereby receives exactly 64 patches, and the patch counts agree with patch_first and patch_of_byte. `w_qkv`: independent entries of order 1024 ** -0.5. `byte_states`: entries of order one.
All inputs are finite; a program needn't handle non-finite values.
Results may differ from a plain program's by a relative error of at most 0.011.
Values may be sent and summed in bfloat16 or wider, within the bound.
A program may use at most 64 MiB of HBM per device.

v0:
```python
import jax
import jax.numpy as jnp
from jax import lax
from jax.sharding import PartitionSpec as P

HD = 128


def extended_2(x, sides, width):
    for axis, dim in sides:
        peers, length = (lax.axis_size(axis), x.shape[dim])
        up = [(i, (i + 1) % peers) for i in range(peers - 1)]
        down = [(j, i) for i, j in up]
        last = lax.slice_in_dim(x, length - width, length, axis=dim)
        first = lax.slice_in_dim(x, 0, width, axis=dim)
        before = lax.ppermute(last, axis, up)
        after = lax.ppermute(first, axis, down)
        x = jnp.concatenate([before, x, after], axis=dim)
    return x


def pick_own(values, index):
    return lax.dynamic_index_in_dim(values, index, 0, keepdims=False)


def shards(byte_states, patch_of_byte, patch_first, moved, w_qkv, d_attn):
    ctx_index = lax.axis_index("ctx")
    n_ctx = lax.axis_size("ctx")
    rows = d_attn.shape[0]
    feats = d_attn.shape[1]
    heads = feats // HD
    capacity = 2 * rows
    total = rows * n_ctx
    scale = HD ** (-0.5)
    ends = jnp.concatenate([patch_first[1:], jnp.full((1,), total, jnp.int32)])
    counts = ends - patch_first
    lower_moves = moved[0]
    upper_moves = moved[1]
    zero_one = jnp.zeros((1,), jnp.int32)
    below_high = jnp.concatenate([zero_one, upper_moves[:-1]])
    above_low = jnp.concatenate([lower_moves[1:], zero_one])
    prev_first = jnp.concatenate([zero_one, patch_first[:-1]])
    prev_count = jnp.concatenate([zero_one, counts[:-1]])
    ranks = jnp.arange(rows, dtype=jnp.int32)[None, :]
    from_low = ranks < below_high[:, None]
    from_high = ranks >= (rows - above_low)[:, None]
    lower_local = prev_count[:, None] - below_high[:, None] + ranks
    own_local = lower_moves[:, None] + ranks - below_high[:, None]
    upper_local = ranks - (rows - above_low)[:, None]
    ids_all = jnp.where(
        from_low,
        prev_first[:, None] + lower_local,
        jnp.where(from_high, ends[:, None] + upper_local, patch_first[:, None] + own_local),
    )
    source_all = jnp.where(
        from_low,
        lower_local,
        jnp.where(from_high, 2 * capacity + upper_local, capacity + own_local),
    )
    wanted = pick_own(ids_all, ctx_index)
    source_rows = pick_own(source_all, ctx_index)
    key_place = ids_all.reshape(-1)
    slots = jnp.arange(capacity, dtype=jnp.int32)
    member = patch_of_byte[None, :] == slots[:, None]
    lengths = jnp.sum(member.astype(jnp.float32), axis=1)
    onehot = member.astype(jnp.bfloat16)
    part = byte_states.shape[1] // lax.axis_size("tp")
    source = lax.dynamic_slice_in_dim(byte_states, lax.axis_index("tp") * part, part, 1)
    pooled_local = (
        jnp.dot(onehot, source, preferred_element_type=jnp.float32)
        / jnp.maximum(lengths, 1.0)[:, None]
    ).astype(jnp.bfloat16)
    extended = extended_2(pooled_local, (("ctx", 0),), capacity)
    picker = (source_rows[:, None] == jnp.arange(3 * capacity, dtype=jnp.int32)[None, :]).astype(
        jnp.bfloat16
    )
    pooled = jnp.dot(picker, extended, preferred_element_type=jnp.float32).astype(jnp.bfloat16)
    pooled = lax.all_gather(pooled, "tp", axis=1, tiled=True)
    query = jnp.dot(pooled, w_qkv[0], preferred_element_type=jnp.float32).astype(jnp.bfloat16)
    keyed = jnp.dot(pooled, w_qkv[1], preferred_element_type=jnp.float32).astype(jnp.bfloat16)
    valued = jnp.dot(pooled, w_qkv[2], preferred_element_type=jnp.float32).astype(jnp.bfloat16)
    keys_all, values_all = (
        lax.all_gather(keyed, "ctx", axis=0, tiled=True),
        lax.all_gather(valued, "ctx", axis=0, tiled=True),
    )
    query3 = query.reshape(rows, heads, HD)
    keys3 = keys_all.reshape(total, heads, HD)
    values3 = values_all.reshape(total, heads, HD)
    causal = (wanted[:, None] >= key_place[None, :])[None, :, :]
    score = jnp.einsum("qhd,khd->hqk", query3, keys3, preferred_element_type=jnp.float32) * scale
    masked = jnp.where(causal, score, -jnp.inf)
    top = jnp.max(masked, axis=2, keepdims=True)
    lse = top + jnp.log(jnp.sum(jnp.exp(masked - top), axis=2, keepdims=True))
    prob = jnp.exp(jnp.where(causal, score - lse, -jnp.inf))
    probs = prob.astype(jnp.bfloat16)
    output3 = jnp.einsum("hqk,khd->qhd", probs, values3, preferred_element_type=jnp.float32).astype(
        jnp.bfloat16
    )
    attn_out = output3.reshape(rows, feats)
    grad3 = d_attn.reshape(rows, heads, HD)
    delta = jnp.sum(grad3.astype(jnp.float32) * output3.astype(jnp.float32), axis=2)
    dprob = jnp.einsum("qhd,khd->hqk", grad3, values3, preferred_element_type=jnp.float32)
    dscore = (prob * (dprob - jnp.transpose(delta)[:, :, None])).astype(jnp.bfloat16)
    d_query = (
        jnp.einsum("hqk,khd->qhd", dscore, keys3, preferred_element_type=jnp.float32) * scale
    ).astype(jnp.bfloat16)
    lse_rows = jnp.transpose(lse[:, :, 0])
    lse_all, delta_all = (
        lax.all_gather(lse_rows, "ctx", axis=0, tiled=True),
        lax.all_gather(delta, "ctx", axis=0, tiled=True),
    )
    own_keys = keyed.reshape(rows, heads, HD)
    own_values = valued.reshape(rows, heads, HD)
    q_piece = lax.all_gather(query, "ctx", axis=0, tiled=True)
    g_piece = lax.all_gather(d_attn, "ctx", axis=0, tiled=True)
    count = q_piece.shape[0]
    q_three = q_piece.reshape(count, heads, HD)
    g_three = g_piece.reshape(count, heads, HD)
    lse_piece = jnp.transpose(lse_all)
    delta_piece = jnp.transpose(delta_all)
    allowed = (key_place[:, None] >= wanted[None, :])[None, :, :]
    part_score = (
        jnp.einsum("qhd,khd->hqk", q_three, own_keys, preferred_element_type=jnp.float32) * scale
    )
    part_prob = jnp.exp(jnp.where(allowed, part_score - lse_piece[:, :, None], -jnp.inf))
    part_probs = part_prob.astype(jnp.bfloat16)
    d_value_sum = jnp.einsum(
        "hqk,qhd->khd", part_probs, g_three, preferred_element_type=jnp.float32
    )
    part_dprob = jnp.einsum("qhd,khd->hqk", g_three, own_values, preferred_element_type=jnp.float32)
    part_dscore = (part_prob * (part_dprob - delta_piece[:, :, None])).astype(jnp.bfloat16)
    d_key_sum = (
        jnp.einsum("hqk,qhd->khd", part_dscore, q_three, preferred_element_type=jnp.float32) * scale
    )
    d_key_sum, d_value_sum = (d_key_sum, d_value_sum)
    d_key = d_key_sum.astype(jnp.bfloat16).reshape(rows, feats)
    d_value = d_value_sum.astype(jnp.bfloat16).reshape(rows, feats)
    d_query = d_query.reshape(rows, feats)
    contract = (((1,), (1,)), ((), ()))
    partial_value = lax.dot_general(d_query, w_qkv[0], contract, preferred_element_type=jnp.float32)
    partial_value = partial_value + lax.dot_general(
        d_key, w_qkv[1], contract, preferred_element_type=jnp.float32
    )
    partial_value = partial_value + lax.dot_general(
        d_value, w_qkv[2], contract, preferred_element_type=jnp.float32
    )
    d_pooled = lax.psum_scatter(partial_value, "tp", scatter_dimension=1, tiled=True).astype(
        jnp.bfloat16
    )
    returned = extended_2(d_pooled, (("ctx", 0),), rows)
    my_count = pick_own(counts, ctx_index)
    my_low = pick_own(lower_moves, ctx_index)
    my_high = pick_own(upper_moves, ctx_index)
    my_below = pick_own(below_high, ctx_index)
    target = jnp.where(
        patch_of_byte < my_low,
        rows - my_low + patch_of_byte,
        jnp.where(
            patch_of_byte >= my_count - my_high,
            2 * rows + patch_of_byte - (my_count - my_high),
            rows + my_below + patch_of_byte - my_low,
        ),
    )
    chooser = (target[:, None] == jnp.arange(3 * rows, dtype=jnp.int32)[None, :]).astype(
        jnp.bfloat16
    )
    spread_back = jnp.dot(chooser, returned, preferred_element_type=jnp.float32)
    byte_lengths = jnp.sum(jnp.where(member, lengths[:, None], 0.0), axis=0)
    byte_grad = (spread_back / byte_lengths[:, None]).astype(jnp.bfloat16)
    return (attn_out, byte_grad)


def solution(mesh):
    placed = (P("ctx", None), P("ctx"), P(), P(), P(None, None, "tp"), P("ctx", "tp"))
    return jax.shard_map(
        shards,
        mesh=mesh,
        in_specs=placed,
        out_specs=(P("ctx", "tp"), P("ctx", "tp")),
        check_vma=False,
    )
```

profile of v0, /device:TPU:6, one launch (start us, length us, event | category | flops | bytes accessed | tf_op | source)
XLA Modules:
  0.0 305.7 jit_solution(10949627991634043434)
XLA Ops:
  7.2 0.7 all-gather.13.cloned.1.call-update
  8.0 0.8 convert_reduce_fusion
  8.8 0.9 fusion.56
  9.7 3.4 %collective-permute-start = (bf16[128,512]{1,0:T(8,128)(2,1)S(1)}, bf16[128,512]{1,0:T(8,128)(2,1)S(1)}, u32[]{:S(2)}, u32[]{:S(2)}) collective-permute-start(bf16[128,512]{1,0:T(8,128)(2,1)S(1)} %fusion.56), channel_id=1, source_target_pairs={{0,2},{2,4},{4,6},{6,8},{8,10},{10,12},{12,14},{14,16},{16,18},{18... | collective-permute-start | bytes 393224 | tf_op jit(solution)/shard_map/ppermute | solution.py:16
  13.1 2.4 collective-permute-start.1
  15.5 0.8 slice_bitcast_fusion.1
  16.4 0.8 fusion.133
  17.2 0.7 pad_add_fusion.3
  18.0 0.8 fusion.132
  19.2 1.2 dynamic-slice.3
  20.4 0.6 dynamic-slice.4
  21.0 0.6 dynamic-slice.2
  21.6 1.9 select_bitcast_fusion
  23.5 0.2 convolution_convert_fusion.1
  23.8 1.9 all_gather.21
  25.7 2.7 fusion.66
  28.5 2.7 fusion.60
  31.3 2.7 fusion.63
  35.4 36.0 %all-gather.13.cloned.1.call-done = bf16[1024,1024]{1,0:T(8,128)(2,1)} async-done(((bf16[64,1024]{1,0:T(8,128)(2,1)}), bf16[1024,1024]{1,0:T(8,128)(2,1)}) %all-gather.13.cloned.1.call-update) | async-done | bytes 2097168 | tf_op jit(solution)/shard_map/all_gather | solution.py:115
  71.4 2.9 copy.61
  74.3 59.7 %all-gather.9.cloned.1.call-done = bf16[1024,1024]{1,0:T(8,128)(2,1)} async-done(((bf16[64,1024]{1,0:T(8,128)(2,1)}), bf16[1024,1024]{1,0:T(8,128)(2,1)}) %all-gather.9.cloned.1.call-update) | async-done | bytes 2097168 | tf_op jit(solution)/shard_map/all_gather | solution.py:83
  134.0 2.6 select_reduce_fusion
  136.6 1.3 copy-done.2
  137.9 0.6 exponential_reduce_fusion
  138.5 33.8 %all-gather = f32[16,64,8]{1,2,0:T(8,128)S(1)} all-gather(f32[1,64,8]{1,2,0:T(8,128)S(1)} %bitcast.202), channel_id=1, replica_groups=mesh['ctx'=16,'tp'=2] {'ctx'}, dimensions={0}, use_global_device_ids=true | all-gather | bytes 34816 | tf_op jit(solution)/shard_map/all_gather | solution.py:109
  172.4 23.7 %all-gather.7.cloned.1.call-done = bf16[1024,1024]{1,0:T(8,128)(2,1)} async-done(((bf16[64,1024]{1,0:T(8,128)(2,1)}), bf16[1024,1024]{1,0:T(8,128)(2,1)}) %all-gather.7.cloned.1.call-update) | async-done | bytes 2097168 | tf_op jit(solution)/shard_map/all_gather | solution.py:84
  196.2 3.8 %multiply_reduce_fusion = (f32[64,8]{0,1:T(8,128)S(1)}, bf16[8,128,64]{1,2,0:T(8,128)(2,1)}) fusion(f32[8,64,1024]{2,1,0:T(8,128)} %copy-done.2, f32[8,64]{1,0:T(8,128)S(1)} %log_add_fusion, pred[64,1024]{1,0:T(8,128)(4,1)S(1)} %broadcast_compare_fusion.1, bf16[1024,1024]{1,0:T(8,128)(2,1)} %all-gather.7.cloned.1.call-done, bf16[64,1024]{1,0:T(8,128)(2,1)S(1)} %copy-done.6), kind=kOutput, calls=%fused_computation.75 | convolution fusion | flops 136642048 | bytes 4526080 | tf_op jit(solution)/shard_map/hqk,khd->qhd/dot_general | solution.py:96
  200.0 33.9 %all-gather.1 = f32[16,64,8]{1,2,0:T(8,128)S(1)} all-gather(f32[1,64,8]{1,2,0:T(8,128)S(1)} %bitcast.203), channel_id=1, replica_groups=mesh['ctx'=16,'tp'=2] {'ctx'}, dimensions={0}, use_global_device_ids=true | all-gather | bytes 34816 | tf_op jit(solution)/shard_map/all_gather | solution.py:110
  233.9 24.8 %all-gather.11.cloned.1.call-done = bf16[1024,1024]{1,0:T(8,128)(2,1)} async-done(((bf16[64,1024]{1,0:T(8,128)(2,1)}), bf16[1024,1024]{1,0:T(8,128)(2,1)}) %all-gather.11.cloned.1.call-update) | async-done | bytes 2097168 | tf_op jit(solution)/shard_map/all_gather | solution.py:114
  258.7 2.7 select_exponential_fusion
  261.4 0.9 fusion.78
  262.3 0.5 copy-done.1
  262.8 3.3 %fusion.75 = bf16[8,8,8,128]{3,2,1,0:T(8,128)(2,1)S(1)} fusion(f32[8,1024,64]{1,2,0:T(8,128)} %copy-done.1, bf16[1024,8,128]{0,2,1:T(8,128)(2,1)S(1)} %bitcast.199, f32[8,1024]{1,0:T(8,128)S(1)} %bitcast.200, bf16[1024,1024]{1,0:T(8,128)(2,1)} %all-gather.11.cloned.1.call-done, bf16[64,1024]{1,0:T(8,128)(2,1)S(1)} %copy-done.4), kind=kOutput, calls=%fused_computation.60 | convolution fusion | flops 270139392 | bytes 6586368 | tf_op jit(solution)/shard_map/hqk,qhd->khd/dot_general | solution.py:133
  266.1 2.5 fusion.14
  268.6 4.0 %fusion.79 = bf16[8,8,8,128]{3,2,1,0:T(8,128)(2,1)S(1)} fusion(f32[8,64,1024]{2,1,0:T(8,128)S(1)} %copy-done.3, f32[8,64]{1,0:T(8,128)S(1)} %bitcast.204, f32[8,64]{1,0:T(8,128)S(1)} %log_add_fusion, pred[64,1024]{1,0:T(8,128)(4,1)S(1)} %broadcast_compare_fusion.1, bf16[1024,1024]{1,0:T(8,128)(2,1)} %all-gather.7.cloned.1.call-done, ...), kind=kOutput, calls=%fused_computation.62 | convolution fusion | flops 271712256 | bytes 6623232 | tf_op jit(solution)/shard_map/hqk,khd->qhd/dot_general | solution.py:105
  272.6 2.4 fusion.47
  275.0 3.1 %fusion.44 = f32[64,1024]{1,0:T(8,128)} fusion(f32[64,1024]{1,0:T(8,128)S(1)} %fusion.47, bf16[3,1024,1024]{2,1,0:T(8,128)(2,1)} %param.10, bf16[8,8,8,128]{3,2,1,0:T(8,128)(2,1)S(1)} %fusion.78), kind=kOutput, calls=%fused_computation.47 | convolution fusion | flops 134283264 | bytes 2752512 | tf_op jit(solution)/shard_map/dot_general | solution.py:144
  278.1 0.6 dynamic_slice.27
  278.7 0.6 dynamic_slice.29
  279.3 0.7 constant_dynamic-slice_fusion.3
  282.7 0.7 compare_select_fusion.1
  283.4 2.6 reduce-scatter.2.cloned.1.call-done
  285.9 0.9 convert_element_type.89
  286.9 3.4 %collective-permute-start.2 = (bf16[64,512]{1,0:T(8,128)(2,1)S(1)}, bf16[64,512]{1,0:T(8,128)(2,1)S(1)}, u32[]{:S(2)}, u32[]{:S(2)}) collective-permute-start(bf16[64,512]{1,0:T(8,128)(2,1)S(1)} %convert_element_type.89), channel_id=1, source_target_pairs={{0,2},{2,4},{4,6},{6,8},{8,10},{10,12},{12,14},{14,16},{16,18},{18... | collective-permute-start | bytes 196616 | tf_op jit(solution)/shard_map/ppermute | solution.py:16
  290.2 2.5 collective-permute-start.3
  292.7 0.7 copy_bitcast_fusion
  293.4 4.8 %collective-permute-done.3 = bf16[64,512]{1,0:T(8,128)(2,1)S(1)} collective-permute-done((bf16[64,512]{1,0:T(8,128)(2,1)S(1)}, bf16[64,512]{1,0:T(8,128)(2,1)S(1)}, u32[]{:S(2)}, u32[]{:S(2)}) %collective-permute-start.3) | collective-permute-done | bytes 65568 | tf_op jit(solution)/shard_map/ppermute | solution.py:17
  298.2 1.0 fusion.43
  (65 shorter events, 2.5 us)
Async XLA Ops:
  7.2 1.6 copy-start
  7.2 64.3 %all-gather.13.cloned.1.call-start = ((), (), s32[]{:S(2)}) async-start(), calls=%async_computation.4 | async-start | bytes 2228224 | tf_op jit(solution)/shard_map/all_gather | solution.py:115
  7.9 126.1 %all-gather.9.cloned.1.call-start = ((), (), s32[]{:S(2)}) async-start(), calls=%async_computation.2 | async-start | bytes 2228224 | tf_op jit(solution)/shard_map/all_gather | solution.py:83
  9.7 13.9 %collective-permute-start = (bf16[128,512]{1,0:T(8,128)(2,1)S(1)}, bf16[128,512]{1,0:T(8,128)(2,1)S(1)}, u32[]{:S(2)}, u32[]{:S(2)}) collective-permute-start(bf16[128,512]{1,0:T(8,128)(2,1)S(1)} %fusion.56), channel_id=1, source_target_pairs={{0,2},{2,4},{4,6},{6,8},{8,10},{10,12},{12,14},{14,16},{16,18},{18... | collective-permute-start | bytes 393224 | tf_op jit(solution)/shard_map/ppermute | solution.py:16
  13.1 10.5 %collective-permute-start.1 = (bf16[128,512]{1,0:T(8,128)(2,1)S(1)}, bf16[128,512]{1,0:T(8,128)(2,1)S(1)}, u32[]{:S(2)}, u32[]{:S(2)}) collective-permute-start(bf16[128,512]{1,0:T(8,128)(2,1)S(1)} %fusion.56), channel_id=1, source_target_pairs={{2,0},{4,2},{6,4},{8,6},{10,8},{12,10},{14,12},{16,14},{18,16},{20... | collective-permute-start | bytes 393224 | tf_op jit(solution)/shard_map/ppermute | solution.py:17
  28.4 167.7 %all-gather.7.cloned.1.call-start = ((), (), s32[]{:S(2)}) async-start(), calls=%async_computation.1 | async-start | bytes 2228224 | tf_op jit(solution)/shard_map/all_gather | solution.py:84
  31.2 3.7 %copy-start.9 = (s32[16]{0:T(128)S(1)}, s32[16]{0:T(128)}, u32[]{:S(2)}) copy-start(s32[16]{0:T(128)} %param.8) | copy-start | bytes 196
  31.2 227.5 %all-gather.11.cloned.1.call-start = ((), (), s32[]{:S(2)}) async-start(), calls=%async_computation.3 | async-start | bytes 2228224 | tf_op jit(solution)/shard_map/all_gather | solution.py:114
  34.0 251.9 %reduce-scatter.2.cloned.1.call-start = ((), (), s32[]{:S(2)}) async-start(), calls=%async_computation.5 | async-start | bytes 393216 | tf_op jit(solution)/shard_map/reduce_scatter | solution.py:147
  35.4 98.6 %copy-start.5 = (bf16[64,1024]{1,0:T(8,128)(2,1)S(1)}, bf16[64,1024]{1,0:T(8,128)(2,1)}, u32[]{:S(2)}) copy-start(bf16[64,1024]{1,0:T(8,128)(2,1)} %fusion.63) | copy-start | bytes 393220
  136.6 1.4 copy-start.2
  136.6 59.6 %copy-start.6 = (bf16[64,1024]{1,0:T(8,128)(2,1)S(1)}, bf16[64,1024]{1,0:T(8,128)(2,1)}, u32[]{:S(2)}) copy-start(bf16[64,1024]{1,0:T(8,128)(2,1)} %param.11) | copy-start | bytes 393220
  172.4 86.3 %copy-start.7 = (bf16[64,1024]{1,0:T(8,128)(2,1)S(1)}, bf16[64,1024]{1,0:T(8,128)(2,1)}, u32[]{:S(2)}) copy-start(bf16[64,1024]{1,0:T(8,128)(2,1)} %fusion.66) | copy-start | bytes 393220
  261.4 1.4 copy-start.1
  261.4 1.4 copy-start.4
  266.1 2.5 copy-start.3
  275.0 7.6 %copy-start.10 = (s32[256]{0:T(256)S(1)}, s32[256]{0:T(256)}, u32[]{:S(2)}) copy-start(s32[256]{0:T(256)} %param.7) | copy-start | bytes 3076
  275.0 17.7 %copy-start.8 = (bf16[8,128,64]{1,2,0:T(8,128)(2,1)S(1)}, bf16[8,128,64]{1,2,0:T(8,128)(2,1)}, u32[]{:S(2)}) copy-start(bf16[8,128,64]{1,2,0:T(8,128)(2,1)} %get-tuple-element.18) | copy-start | bytes 393220
  286.9 6.5 %collective-permute-start.2 = (bf16[64,512]{1,0:T(8,128)(2,1)S(1)}, bf16[64,512]{1,0:T(8,128)(2,1)S(1)}, u32[]{:S(2)}, u32[]{:S(2)}) collective-permute-start(bf16[64,512]{1,0:T(8,128)(2,1)S(1)} %convert_element_type.89), channel_id=1, source_target_pairs={{0,2},{2,4},{4,6},{6,8},{8,10},{10,12},{12,14},{14,16},{16,18},{18... | collective-permute-start | bytes 196616 | tf_op jit(solution)/shard_map/ppermute | solution.py:16
  290.2 8.0 %collective-permute-start.3 = (bf16[64,512]{1,0:T(8,128)(2,1)S(1)}, bf16[64,512]{1,0:T(8,128)(2,1)S(1)}, u32[]{:S(2)}, u32[]{:S(2)}) collective-permute-start(bf16[64,512]{1,0:T(8,128)(2,1)S(1)} %convert_element_type.89), channel_id=1, source_target_pairs={{2,0},{4,2},{6,4},{8,6},{10,8},{12,10},{14,12},{16,14},{18,16},{20... | collective-permute-start | bytes 196616 | tf_op jit(solution)/shard_map/ppermute | solution.py:17
Sparse Core Ops, SparseCore 0:
  10.8 60.6 all-gather.12
  74.8 59.1 all-gather.8
  136.8 59.3 all-gather.6
  199.4 59.2 all-gather.10
  278.3 7.6 reduce-scatter.1
where the time goes:
time: 306 us
  waiting for transfers between devices  152 us (50%)
  blocking collectives  69.5 us (23%)
  matrix products  35.5 us (12%)
  between operations  16.7 us (5%)
  local copies, waits for them, and re-layouts  13.3 us (4%)
  starting transfers between devices  11.9 us (4%)
  other arithmetic  6.49 us (2%)
    all_gather x1, waiting for transfers between devices, shards(): lax.all_gather(keyed, 'ctx', axis=0, tiled=True)  59.7 us
    all_gather x1, waiting for transfers between devices, shards(): g_piece = lax.all_gather(d_attn, 'ctx', axis=0, tiled=True)  36 us
    all_gather x1, blocking collectives, shards(): lax.all_gather(delta, 'ctx', axis=0, tiled=True)  33.9 us
    all_gather x1, blocking collectives, shards(): lax.all_gather(lse_rows, 'ctx', axis=0, tiled=True)  33.8 us
    all_gather x1, waiting for transfers between devices, shards(): q_piece = lax.all_gather(query, 'ctx', axis=0, tiled=True)  24.8 us
    all_gather x1, waiting for transfers between devices, shards(): lax.all_gather(valued, 'ctx', axis=0, tiled=True)  23.7 us
    ppermute x2, starting transfers between devices, extended_2(): before = lax.ppermute(last, axis, up)  6.77 us
  transfers between devices with their start and end apart: 9, of which 6 were waited for; matrix products, arithmetic and copies ran while one was open for 11% of the time, Pallas kernels for 0%

commit v1 on v0

--- a/solution.py
+++ b/solution.py
@@ -112,7 +112,9 @@
     own_keys = keyed.reshape(rows, heads, HD)
     own_values = valued.reshape(rows, heads, HD)
     q_piece = lax.all_gather(query, "ctx", axis=0, tiled=True)
-    g_piece = lax.all_gather(d_attn, "ctx", axis=0, tiled=True)
+    g_piece = jnp.concatenate(
+        lax.all_to_all(jnp.stack([d_attn] * lax.axis_size("ctx")), "ctx", 0, 0), axis=0
+    )
     count = q_piece.shape[0]
     q_three = q_piece.reshape(count, heads, HD)
     g_three = g_piece.reshape(count, heads, HD)

time: 306 us -> 281 us (0.918)
  waiting for transfers between devices: 152 us -> 117 us
  starting transfers between devices: 11.9 us -> 19.1 us
    all_to_all x0 -> x1, waiting for transfers between devices: none -> 46.8 us  [shards(): lax.all_to_all(jnp.stack([d_attn] * lax.axis_size('ctx')), 'ctx', 0, 0)]
    all_gather x1, waiting for transfers between devices: 59.7 us -> 14.2 us  [shards(): lax.all_gather(keyed, 'ctx', axis=0, tiled=True)]
    all_gather x1 -> x0, waiting for transfers between devices: 36 us -> none  [shards(): g_piece = lax.all_gather(d_attn, 'ctx', axis=0, tiled=True)]
    all_to_all x0 -> x1, starting transfers between devices: none -> 7.25 us  [shards(): lax.all_to_all(jnp.stack([d_attn] * lax.axis_size('ctx')), 'ctx', 0, 0)]
    unnamed x24 -> x27, local copies, waits for them, and re-layouts: 2.04 us -> 5.88 us
  transfers between devices with their start and end apart: 9 -> 9, of which waited for: 6 -> 6; matrix products, arithmetic and copies ran while one was open for 11% -> 10% of each run, Pallas kernels for 0% -> 0%
where the time goes in v1:
time: 281 us
  waiting for transfers between devices  117 us (42%)
  blocking collectives  70.1 us (25%)
  matrix products  35.8 us (13%)
  starting transfers between devices  19.1 us (7%)
  between operations  16.6 us (6%)
  local copies, waits for them, and re-layouts  16 us (6%)
  other arithmetic  6.54 us (2%)
    all_to_all x1, waiting for transfers between devices, shards(): lax.all_to_all(jnp.stack([d_attn] * lax.axis_size('ctx')), 'ctx', 0, 0)  46.8 us
    all_gather x1, blocking collectives, shards(): lax.all_gather(lse_rows, 'ctx', axis=0, tiled=True)  34.1 us
    all_gather x1, blocking collectives, shards(): lax.all_gather(delta, 'ctx', axis=0, tiled=True)  34 us
    all_gather x1, waiting for transfers between devices, shards(): q_piece = lax.all_gather(query, 'ctx', axis=0, tiled=True)  24.7 us
    all_gather x1, waiting for transfers between devices, shards(): lax.all_gather(valued, 'ctx', axis=0, tiled=True)  23.4 us
    all_gather x1, waiting for transfers between devices, shards(): lax.all_gather(keyed, 'ctx', axis=0, tiled=True)  14.2 us
    all_to_all x1, starting transfers between devices, shards(): lax.all_to_all(jnp.stack([d_attn] * lax.axis_size('ctx')), 'ctx', 0, 0)  7.25 us
    ppermute x2, starting transfers between devices, extended_2(): before = lax.ppermute(last, axis, up)  6.77 us
  transfers between devices with their start and end apart: 9, of which 6 were waited for; matrix products, arithmetic and copies ran while one was open for 10% of the time, Pallas kernels for 0%

profile of v1, /device:TPU:6, one launch (start us, length us, event | category | flops | bytes accessed | tf_op | source)
XLA Modules:
  0.0 280.7 jit_solution(2057146116143918981)
XLA Ops:
  7.2 0.8 convert_reduce_fusion
  8.2 0.9 fusion.71
  9.1 3.4 %collective-permute-start = (bf16[128,512]{1,0:T(8,128)(2,1)S(1)}, bf16[128,512]{1,0:T(8,128)(2,1)S(1)}, u32[]{:S(2)}, u32[]{:S(2)}) collective-permute-start(bf16[128,512]{1,0:T(8,128)(2,1)S(1)} %fusion.71), channel_id=1, source_target_pairs={{0,2},{2,4},{4,6},{6,8},{8,10},{10,12},{12,14},{14,16},{16,18},{18... | collective-permute-start | bytes 393224 | tf_op jit(solution)/shard_map/ppermute | solution.py:16
  12.5 2.4 collective-permute-start.1
  15.0 0.8 slice_bitcast_fusion.1
  15.8 0.8 fusion.151
  16.5 0.8 fusion.152
  17.3 0.7 pad_add_fusion.3
  18.6 1.2 dynamic-slice.3
  19.9 0.6 dynamic-slice.4
  20.4 0.6 dynamic-slice.2
  21.0 1.9 select_bitcast_fusion
  23.2 1.9 all_gather.18
  25.1 2.8 fusion.81
  28.0 2.7 fusion.75
  30.7 1.6 stack.2
  32.3 7.3 %all-to-all-start = ((bf16[16,64,1024]{2,1,0:T(8,128)(2,1)}), bf16[16,64,1024]{2,1,0:T(8,128)(2,1)S(1)}, u32[]{:S(2)}, u32[]{:S(2)}) async-start(bf16[16,64,1024]{2,1,0:T(8,128)(2,1)} %stack.2), calls=%async_computation | async-start | bytes 4194304 | tf_op jit(solution)/shard_map/all_to_all | solution.py:116
  39.7 2.7 fusion.78
  43.8 46.8 %all-to-all-done = bf16[16,64,1024]{2,1,0:T(8,128)(2,1)S(1)} async-done(((bf16[16,64,1024]{2,1,0:T(8,128)(2,1)}), bf16[16,64,1024]{2,1,0:T(8,128)(2,1)S(1)}, u32[]{:S(2)}, u32[]{:S(2)}) %all-to-all-start) | async-done | bytes 2097184 | tf_op jit(solution)/shard_map/all_to_all | solution.py:116
  90.5 1.4 copy-done.4
  91.9 2.2 copy.77
  94.2 14.2 %all-gather.8.cloned.1.call-done = bf16[1024,1024]{1,0:T(8,128)(2,1)} async-done(((bf16[64,1024]{1,0:T(8,128)(2,1)}), bf16[1024,1024]{1,0:T(8,128)(2,1)}) %all-gather.8.cloned.1.call-update) | async-done | bytes 2097168 | tf_op jit(solution)/shard_map/all_gather | solution.py:83
  108.3 2.6 select_reduce_fusion
  110.9 1.4 copy-done.2
  112.3 0.6 exponential_reduce_fusion
  112.9 34.1 %all-gather = f32[16,64,8]{1,2,0:T(8,128)S(1)} all-gather(f32[1,64,8]{1,2,0:T(8,128)S(1)} %bitcast.203), channel_id=1, replica_groups=mesh['ctx'=16,'tp'=2] {'ctx'}, dimensions={0}, use_global_device_ids=true | all-gather | bytes 34816 | tf_op jit(solution)/shard_map/all_gather | solution.py:109
  147.1 23.4 %all-gather.6.cloned.1.call-done = bf16[1024,1024]{1,0:T(8,128)(2,1)} async-done(((bf16[64,1024]{1,0:T(8,128)(2,1)}), bf16[1024,1024]{1,0:T(8,128)(2,1)}) %all-gather.6.cloned.1.call-update) | async-done | bytes 2097168 | tf_op jit(solution)/shard_map/all_gather | solution.py:84
  170.6 3.8 %multiply_reduce_fusion = (f32[64,8]{0,1:T(8,128)S(1)}, bf16[8,128,64]{1,2,0:T(8,128)(2,1)}) fusion(f32[8,64,1024]{2,1,0:T(8,128)} %copy-done.2, f32[8,64]{1,0:T(8,128)S(1)} %log_add_fusion, pred[64,1024]{1,0:T(8,128)(4,1)S(1)} %broadcast_compare_fusion.1, bf16[1024,1024]{1,0:T(8,128)(2,1)} %all-gather.6.cloned.1.call-done, bf16[64,1024]{1,0:T(8,128)(2,1)S(1)} %copy-done.7), kind=kOutput, calls=%fused_computation.79 | convolution fusion | flops 136642048 | bytes 4526080 | tf_op jit(solution)/shard_map/hqk,khd->qhd/dot_general | solution.py:96
  174.4 34.0 %all-gather.1 = f32[16,64,8]{1,2,0:T(8,128)S(1)} all-gather(f32[1,64,8]{1,2,0:T(8,128)S(1)} %bitcast.204), channel_id=1, replica_groups=mesh['ctx'=16,'tp'=2] {'ctx'}, dimensions={0}, use_global_device_ids=true | all-gather | bytes 34816 | tf_op jit(solution)/shard_map/all_gather | solution.py:110
  208.5 24.7 %all-gather.10.cloned.1.call-done = bf16[1024,1024]{1,0:T(8,128)(2,1)} async-done(((bf16[64,1024]{1,0:T(8,128)(2,1)}), bf16[1024,1024]{1,0:T(8,128)(2,1)}) %all-gather.10.cloned.1.call-update) | async-done | bytes 2097168 | tf_op jit(solution)/shard_map/all_gather | solution.py:114
  233.2 2.7 select_exponential_fusion
  235.9 0.8 fusion.95
  237.3 3.7 %fusion.90 = bf16[8,8,8,128]{3,2,1,0:T(8,128)(2,1)S(1)} fusion(f32[8,1024,64]{1,2,0:T(8,128)} %copy-done.1, bf16[1024,8,128]{2,1,0:T(8,128)(2,1)S(1)} %bitcast.199, f32[8,1024]{1,0:T(8,128)S(1)} %bitcast.201, bf16[1024,1024]{1,0:T(8,128)(2,1)} %all-gather.10.cloned.1.call-done, bf16[64,1024]{1,0:T(8,128)(2,1)S(1)} %copy-done.5), kind=kOutput, calls=%fused_computation.64 | convolution fusion | flops 270139392 | bytes 6586368 | tf_op jit(solution)/shard_map/hqk,qhd->khd/dot_general | solution.py:135
  241.1 2.5 fusion.14
  243.6 4.0 %fusion.98 = bf16[8,8,8,128]{3,2,1,0:T(8,128)(2,1)S(1)} fusion(f32[8,64,1024]{2,1,0:T(8,128)S(1)} %copy-done.3, f32[8,64]{1,0:T(8,128)S(1)} %bitcast.205, f32[8,64]{1,0:T(8,128)S(1)} %log_add_fusion, pred[64,1024]{1,0:T(8,128)(4,1)S(1)} %broadcast_compare_fusion.1, bf16[1024,1024]{1,0:T(8,128)(2,1)} %all-gather.6.cloned.1.call-done, ...), kind=kOutput, calls=%fused_computation.66 | convolution fusion | flops 271712256 | bytes 6623232 | tf_op jit(solution)/shard_map/hqk,khd->qhd/dot_general | solution.py:105
  247.6 2.4 fusion.55
  250.0 3.1 %fusion.52 = f32[64,1024]{1,0:T(8,128)} fusion(f32[64,1024]{1,0:T(8,128)S(1)} %fusion.55, bf16[3,1024,1024]{2,1,0:T(8,128)(2,1)} %param.10, bf16[8,8,8,128]{3,2,1,0:T(8,128)(2,1)S(1)} %fusion.95), kind=kOutput, calls=%fused_computation.51 | convolution fusion | flops 134283264 | bytes 2752512 | tf_op jit(solution)/shard_map/dot_general | solution.py:146
  253.1 0.6 dynamic_slice.27
  253.7 0.6 dynamic_slice.29
  254.3 0.7 constant_dynamic-slice_fusion.3
  257.6 0.7 compare_select_fusion.1
  258.3 2.6 reduce-scatter.2.cloned.1.call-done
  260.9 0.9 convert_element_type.89
  261.8 3.4 %collective-permute-start.2 = (bf16[64,512]{1,0:T(8,128)(2,1)S(1)}, bf16[64,512]{1,0:T(8,128)(2,1)S(1)}, u32[]{:S(2)}, u32[]{:S(2)}) collective-permute-start(bf16[64,512]{1,0:T(8,128)(2,1)S(1)} %convert_element_type.89), channel_id=1, source_target_pairs={{0,2},{2,4},{4,6},{6,8},{8,10},{10,12},{12,14},{14,16},{16,18},{18... | collective-permute-start | bytes 196616 | tf_op jit(solution)/shard_map/ppermute | solution.py:16
  265.2 2.5 collective-permute-start.3
  267.7 0.7 copy_bitcast_fusion
  268.4 4.8 %collective-permute-done.3 = bf16[64,512]{1,0:T(8,128)(2,1)S(1)} collective-permute-done((bf16[64,512]{1,0:T(8,128)(2,1)S(1)}, bf16[64,512]{1,0:T(8,128)(2,1)S(1)}, u32[]{:S(2)}, u32[]{:S(2)}) %collective-permute-start.3) | collective-permute-done | bytes 65568 | tf_op jit(solution)/shard_map/ppermute | solution.py:17
  273.1 1.0 fusion.51
  (67 shorter events, 3.3 us)
Async XLA Ops:
  7.2 1.1 copy-start
  7.2 101.1 %all-gather.8.cloned.1.call-start = ((), (), s32[]{:S(2)}) async-start(), calls=%async_computation.3 | async-start | bytes 2228224 | tf_op jit(solution)/shard_map/all_gather | solution.py:83
  9.1 13.9 %collective-permute-start = (bf16[128,512]{1,0:T(8,128)(2,1)S(1)}, bf16[128,512]{1,0:T(8,128)(2,1)S(1)}, u32[]{:S(2)}, u32[]{:S(2)}) collective-permute-start(bf16[128,512]{1,0:T(8,128)(2,1)S(1)} %fusion.71), channel_id=1, source_target_pairs={{0,2},{2,4},{4,6},{6,8},{8,10},{10,12},{12,14},{14,16},{16,18},{18... | collective-permute-start | bytes 393224 | tf_op jit(solution)/shard_map/ppermute | solution.py:16
  12.5 10.5 %collective-permute-start.1 = (bf16[128,512]{1,0:T(8,128)(2,1)S(1)}, bf16[128,512]{1,0:T(8,128)(2,1)S(1)}, u32[]{:S(2)}, u32[]{:S(2)}) collective-permute-start(bf16[128,512]{1,0:T(8,128)(2,1)S(1)} %fusion.71), channel_id=1, source_target_pairs={{2,0},{4,2},{6,4},{8,6},{10,8},{12,10},{14,12},{16,14},{18,16},{20... | collective-permute-start | bytes 393224 | tf_op jit(solution)/shard_map/ppermute | solution.py:17
  25.1 5.6 %copy-start.7 = (bf16[64,1024]{1,0:T(8,128)(2,1)S(1)}, bf16[64,1024]{1,0:T(8,128)(2,1)}, u32[]{:S(2)}) copy-start(bf16[64,1024]{1,0:T(8,128)(2,1)} %param.11) | copy-start | bytes 393220
  27.9 142.6 %all-gather.6.cloned.1.call-start = ((), (), s32[]{:S(2)}) async-start(), calls=%async_computation.2 | async-start | bytes 2228224 | tf_op jit(solution)/shard_map/all_gather | solution.py:84
  32.3 58.2 %all-to-all-start = ((bf16[16,64,1024]{2,1,0:T(8,128)(2,1)}), bf16[16,64,1024]{2,1,0:T(8,128)(2,1)S(1)}, u32[]{:S(2)}, u32[]{:S(2)}) async-start(bf16[16,64,1024]{2,1,0:T(8,128)(2,1)} %stack.2), calls=%async_computation | async-start | bytes 4194304 | tf_op jit(solution)/shard_map/all_to_all | solution.py:116
  39.6 3.7 %copy-start.10 = (s32[16]{0:T(128)S(1)}, s32[16]{0:T(128)}, u32[]{:S(2)}) copy-start(s32[16]{0:T(128)} %param.8) | copy-start | bytes 196
  39.6 193.6 %all-gather.10.cloned.1.call-start = ((), (), s32[]{:S(2)}) async-start(), calls=%async_computation.4 | async-start | bytes 2228224 | tf_op jit(solution)/shard_map/all_gather | solution.py:114
  42.4 218.5 %reduce-scatter.2.cloned.1.call-start = ((), (), s32[]{:S(2)}) async-start(), calls=%async_computation.5 | async-start | bytes 393216 | tf_op jit(solution)/shard_map/reduce_scatter | solution.py:149
  90.5 1.4 copy-start.4
  91.9 16.4 %copy-start.6 = (bf16[64,1024]{1,0:T(8,128)(2,1)S(1)}, bf16[64,1024]{1,0:T(8,128)(2,1)}, u32[]{:S(2)}) copy-start(bf16[64,1024]{1,0:T(8,128)(2,1)} %fusion.78) | copy-start | bytes 393220
  110.9 1.4 copy-start.2
  147.1 86.1 %copy-start.8 = (bf16[64,1024]{1,0:T(8,128)(2,1)S(1)}, bf16[64,1024]{1,0:T(8,128)(2,1)}, u32[]{:S(2)}) copy-start(bf16[64,1024]{1,0:T(8,128)(2,1)} %fusion.81) | copy-start | bytes 393220
  235.9 1.4 copy-start.1
  235.9 1.4 copy-start.5
  241.1 2.5 copy-start.3
  249.9 7.6 %copy-start.11 = (s32[256]{0:T(256)S(1)}, s32[256]{0:T(256)}, u32[]{:S(2)}) copy-start(s32[256]{0:T(256)} %param.7) | copy-start | bytes 3076
  249.9 17.7 %copy-start.9 = (bf16[8,128,64]{1,2,0:T(8,128)(2,1)S(1)}, bf16[8,128,64]{1,2,0:T(8,128)(2,1)}, u32[]{:S(2)}) copy-start(bf16[8,128,64]{1,2,0:T(8,128)(2,1)} %get-tuple-element.18) | copy-start | bytes 393220
  261.8 6.5 %collective-permute-start.2 = (bf16[64,512]{1,0:T(8,128)(2,1)S(1)}, bf16[64,512]{1,0:T(8,128)(2,1)S(1)}, u32[]{:S(2)}, u32[]{:S(2)}) collective-permute-start(bf16[64,512]{1,0:T(8,128)(2,1)S(1)} %convert_element_type.89), channel_id=1, source_target_pairs={{0,2},{2,4},{4,6},{6,8},{8,10},{10,12},{12,14},{14,16},{16,18},{18... | collective-permute-start | bytes 196616 | tf_op jit(solution)/shard_map/ppermute | solution.py:16
  265.2 8.0 %collective-permute-start.3 = (bf16[64,512]{1,0:T(8,128)(2,1)S(1)}, bf16[64,512]{1,0:T(8,128)(2,1)S(1)}, u32[]{:S(2)}, u32[]{:S(2)}) collective-permute-start(bf16[64,512]{1,0:T(8,128)(2,1)S(1)} %convert_element_type.89), channel_id=1, source_target_pairs={{2,0},{4,2},{6,4},{8,6},{10,8},{12,10},{14,12},{16,14},{18,16},{20... | collective-permute-start | bytes 196616 | tf_op jit(solution)/shard_map/ppermute | solution.py:17
Sparse Core Ops, SparseCore 0:
  28.0 80.2 all-gather.7
  111.1 59.4 all-gather.5
  173.9 59.2 all-gather.9
  253.2 7.6 reduce-scatter.1
